TPU v7x, 32 devices: a whole 2x2x4 slice. The times are simulated.
32 devices in a mesh: groups: 2 (over x), tile: 8 (over z, y), link: 2 (over core).
Axes of the slice: x: 2, y: 2, z: 4, core: 2. Of those that a mesh axis runs over, the one named last changes fastest.
Arguments:
- points: float32 [9, 30, 2048], P(None, None, ('groups', 'tile')), parts along dimension 2, may hold values from -12 to 12
- potentials: float32 [9, 2048], P(None, ('groups', 'tile')), parts along dimension 1, may hold values from -6 to 124
Outputs:
- residual: float32 [8, 2048], P('link', ('groups', 'tile')), parts along dimension 1
There are 2 independent parts, one for each index of `groups`. A program takes and returns all parts, laid end to end along the dimension named above; each array names one. Nothing has to cross between parts.
All inputs are finite; a program needn't handle non-finite values.
Results may differ from a plain program's by a relative error of at most 0.0003.
Values sent between devices are 32-bit elements; how exact they have to be, the bound alone decides.
A program may use at most 128 MiB of HBM per device.

v0:
```python
import functools
import math

import jax
import jax.numpy as jnp
from jax import lax
from jax.experimental import pallas as pl
from jax.experimental.pallas import tpu as pltpu
from jax.sharding import PartitionSpec as P

EPSILON = 0.5
LOG2E = math.log2(math.e)
SCALE = 2.0 / EPSILON * LOG2E
STRIP = 256
ROWS = 8
BLOCK = 64


def pieces(value):
    high = value.astype(jnp.bfloat16)
    rest = value - high.astype(jnp.float32)
    middle = rest.astype(jnp.bfloat16)
    low = (rest - middle.astype(jnp.float32)).astype(jnp.bfloat16)
    return high, middle, low


def padded(points, extra):
    pad = 32 - points.shape[0]
    row = lax.broadcasted_iota(jnp.int32, (pad, points.shape[1]), 0)
    tail = jnp.where(row == 0, 0.0 if extra is None else extra, 0.0)
    return jnp.concatenate([points, tail], axis=0)


class Chain:
    def __init__(self, links, tiles, pts, pot, right, left, score, alpha, const, rest, col, own, me, time):
        self.links, self.tiles = links, tiles
        self.pts, self.pot = pts, pot
        self.right, self.left, self.score = right, left, score
        self.alpha, self.const, self.rest = alpha, const, rest
        self.col, self.own = col, own
        self.me, self.time = me, time

    def constants(self, k, r):
        t = self.time(k)
        x = self.pts[t, r]
        lanes = pl.ds(pl.multiple_of(r * 128, 128), 128)
        square = jnp.sum(x * x, axis=0, keepdims=True)
        pot = self.pot[r, pl.ds(t, 1), :]
        self.const[t, :, lanes] = (pot - (2.0 / EPSILON) * square) * LOG2E
        if k == 0:
            self.alpha[t, :, lanes] = (pot - square / EPSILON) * LOG2E
        if k == self.links:
            self.rest[:, lanes] = square * (LOG2E / EPSILON)

    def prep_even(self, k, link, r):
        x = self.pts[self.time(k), r]
        one = jnp.full((1, 128), 1.0 if link % 2 == 0 else 0.0, jnp.float32)
        h, m, l = pieces(padded(x, one))
        zero = jnp.zeros_like(h)
        lanes = pl.ds(pl.multiple_of(r * 128, 128), 128)
        self.right[link % 2][:, lanes] = jnp.concatenate([h, h, h, m, l, m, zero, zero], axis=0)

    def prep_odd(self, k, r):
        t = self.time(k)
        lanes = pl.ds(pl.multiple_of(r * 128, 128), 128)
        x = padded(self.pts[t, r] * SCALE, self.const[t, :, lanes])
        h, m, l = pieces(x)
        block = jnp.concatenate([h, m, l, h], axis=0)
        block = block.T
        slot = (k // 2) % 2
        self.left[slot][lanes, 0:128] = block
        self.left[slot][lanes, 128:256] = block

    def prep(self, link, r):
        if link % 2 == 0:
            if link == 0:
                self.constants(0, r)
                self.prep_even(0, link, r)
            else:
                self.prep_even(link, link, r)
            self.constants(link + 1, r)
            self.prep_odd(link + 1, r)
        else:
            self.constants(link + 1, r)
            self.prep_even(link + 1, link, r)

    def product(self, link, i):
        lanes = pl.ds(pl.multiple_of(i * STRIP, STRIP), STRIP)
        slot = (link // 2) % 2
        self.score[link % 2][:, lanes] = jnp.dot(
            self.left[slot][...], self.right[link % 2][:, lanes], preferred_element_type=jnp.float32
        )

    def message(self, link, i):
        t = self.time(link)
        after = self.time(link + 1)
        if link % 2 == 0:
            source = self.alpha[t]
            tiles = [slice(j * 128, (j + 1) * 128) for j in range(self.tiles)]
            for j in range(STRIP // ROWS):
                rows = pl.ds(pl.multiple_of(i * STRIP + j * ROWS, ROWS), ROWS)
                s = [self.score[0][rows, c] + source[:, c] for c in tiles]
                top = functools.reduce(jnp.maximum, s)
                total = functools.reduce(jnp.add, [jnp.exp2(a - top) for a in s])
                peak = jnp.max(top, axis=1, keepdims=True)
                total = jnp.sum(total * jnp.exp2(top - peak), axis=1, keepdims=True)
                out = peak + jnp.log(total) * LOG2E
                self.col[rows, :] = jnp.broadcast_to(out, (ROWS, 128))
        else:
            lanes = pl.ds(pl.multiple_of(i * STRIP, STRIP), STRIP)
            cells = self.col.shape[0]
            step = BLOCK
            peak = total = None
            for j in range(cells // step):
                rows = slice(j * step, (j + 1) * step)
                source = self.col[rows, :]
                s = self.score[1][rows, lanes] + jnp.concatenate([source] * (STRIP // 128), axis=1)
                s = s.reshape(step // 8, 8, STRIP)
                top = jnp.max(s, axis=0)
                if peak is None:
                    peak = top
                    total = jnp.sum(jnp.exp2(s - peak[None]), axis=0)
                else:
                    new = jnp.maximum(peak, top)
                    total = total * jnp.exp2(peak - new) + jnp.sum(jnp.exp2(s - new[None]), axis=0)
                    peak = new
            top = jnp.max(peak, axis=0, keepdims=True)
            total = jnp.sum(total * jnp.exp2(peak - top), axis=0, keepdims=True)
            self.alpha[after, :, lanes] = self.const[after, :, lanes] + top + jnp.log(total) * LOG2E

    def keep(self, k):
        t = self.time(k)
        mine = pl.ds(pl.multiple_of(self.me * 128, 128), 128)
        if k % 2 == 0:
            self.own[t] = self.alpha[t, :, mine]
        else:
            block = self.col[mine, :]
            eye = lax.broadcasted_iota(jnp.int32, (128, 128), 0) == lax.broadcasted_iota(
                jnp.int32, (128, 128), 1
            )
            self.own[t] = jnp.sum(jnp.where(eye, block, 0.0), axis=0, keepdims=True)

    def log_total(self):
        phi = self.alpha[self.time(self.links)] + self.rest[...]
        peak = jnp.max(phi, axis=1, keepdims=True)
        return peak + jnp.log(jnp.sum(jnp.exp2(phi - peak), axis=1, keepdims=True)) * LOG2E

    def loop(self, count, body):
        def turn(i, carry):
            body(i)
            return carry

        lax.fori_loop(0, count, turn, 0)

    def run(self, ready, done):
        turns = self.tiles * 128 // STRIP
        share = self.tiles // turns
        ready(1)
        self.loop(self.tiles, lambda r: self.prep(0, r))
        self.loop(turns, lambda i: self.product(0, i))
        ready(2)
        self.loop(self.tiles, lambda r: self.prep(1, r))
        for link in range(self.links):
            if link + 3 <= self.links:
                ready(link + 3)

            def body(i, link=link):
                self.message(link, i)
                if link + 1 < self.links:
                    self.product(link + 1, i)
                if link + 2 < self.links:
                    for j in range(share):
                        self.prep(link + 2, i * share + j)

            self.loop(turns, body)
            self.keep(link + 1)
            done(link + 1)


def chain_kernel(links, tiles, pts, pot, out, *scratch):
    held, pots, *pairs = scratch[:8]
    right, left, score = pairs[0:2], pairs[2:4], pairs[4:6]
    alpha, const, rest, col, own, other = scratch[8:14]
    line_send, line_recv, pair_send, pair_recv, core_send, core_recv, end_send, end_recv = scratch[14:]
    me = lax.axis_index("tile")
    way = lax.axis_index("link")
    line = tiles // 2
    at, side = me // 2, me % 2
    half = links // 2
    chunks = [(k, 1) for k in range(half + 1)]
    time = lambda k: k + way * (links - 2 * k)
    first = lambda k, count: k + way * (links - 2 * k - count + 1)
    slot = lambda z, y: 2 * z + y
    ahead = lambda d: slot(lax.rem(at + d, line), side)
    behind = lambda d: lax.rem(at + line - d, line)
    chain = Chain(
        links, tiles, held, pots, right, left, score, alpha, const, rest, col, own, me, time
    )

    def fill(t, carry):
        held[t, me] = pts[t]
        return carry

    lax.fori_loop(0, links + 1, fill, 0)
    pots[me] = pot[...]

    barrier = pltpu.get_barrier_semaphore()
    peers = [{"tile": ahead(d)} for d in range(1, line)]
    peers += [{"tile": slot(at, 1 - side)}, {"link": 1 - way}]
    for peer in peers:
        pl.semaphore_signal(barrier, inc=1, device_id=peer)
    pl.semaphore_wait(barrier, len(peers))

    def views(c, origin, source_own):
        if c == 0:
            return (pot if source_own else pots.at[origin]), pots.at[origin]
        k, count = chunks[c - 1]
        span = pl.ds(first(k, count), count)
        return (pts.at[span] if source_own else held.at[span, origin]), held.at[span, origin]

    def remote(c, origin, source_own, send, recv, d, device):
        src, dst = views(c, origin, source_own)
        return pltpu.make_async_remote_copy(
            src_ref=src,
            dst_ref=dst,
            send_sem=send.at[c, d],
            recv_sem=recv.at[c, d],
            device_id=device,
        )

    partner = {"tile": slot(at, 1 - side)}
    sent = []

    def to_line(c, d):
        copy = remote(c, me, True, line_send, line_recv, d, {"tile": ahead(d)})
        copy.start()
        sent.append(copy)

    def to_pair(c, d):
        origin = slot(behind(d), side)
        copy = remote(c, origin, d == 0, pair_send, pair_recv, d, partner)
        copy.start()
        sent.append(copy)

    def forward(c):
        for d in range(1, line):
            origin = slot(behind(d), side)
            remote(c, origin, False, line_send, line_recv, d, partner).wait_recv()
            to_pair(c, d)

    def arrive(c):
        for d in range(line):
            origin = slot(behind(d), 1 - side)
            remote(c, origin, False, pair_send, pair_recv, d, partner).wait_recv()

    def across(k):
        t = time(k)
        copy = pltpu.make_async_remote_copy(
            src_ref=held.at[t],
            dst_ref=held.at[t],
            send_sem=core_send.at[k],
            recv_sem=core_recv.at[k],
            device_id={"link": 1 - way},
        )
        copy.start()
        sent.append(copy)

    def from_core(k):
        t = time(links - k)
        pltpu.make_async_remote_copy(
            src_ref=held.at[t],
            dst_ref=held.at[t],
            send_sem=core_send.at[k],
            recv_sem=core_recv.at[k],
            device_id={"link": 1 - way},
        ).wait_recv()

    def rows(which):
        return pl.ds(first(half, half), half) if which == 0 else pl.ds(time(links), 1)

    def ends(which, span):
        return pltpu.make_async_remote_copy(
            src_ref=own.at[span],
            dst_ref=other.at[span],
            send_sem=end_send.at[which],
            recv_sem=end_recv.at[which],
            device_id={"link": 1 - way},
        )

    for c in range(len(chunks) + 1):
        for d in range(line - 1, 0, -1):
            to_line(c, d)
        to_pair(c, 0)

    def ready(k):
        if k == 1:
            for c in range(4):
                forward(c)
            for c in range(3):
                arrive(c)
            across(1)
            across(0)
        elif k <= half:
            if k < half:
                forward(k + 2)
            arrive(k + 1)
            if k < half:
                across(k)
        else:
            from_core(links - k)

    def done(k):
        if k == links - 1:
            copy = ends(0, rows(0))
            copy.start()
            sent.append(copy)
        if k == links:
            copy = ends(1, rows(1))
            copy.start()
            sent.append(copy)

    chain.run(ready, done)
    chain.keep(0)
    total = chain.log_total()
    ends(0, rows_other(0, links, half, way)).wait_recv()
    ends(1, rows_other(1, links, half, way)).wait_recv()
    mine = pl.ds(pl.multiple_of(me * 128, 128), 128)
    keep = -math.log(tiles * 128)
    for j in range(half):
        t = 1 + way * half + j
        combined = own[t] + other[t] - const[t, :, mine]
        out[pl.ds(j, 1), :] = keep - (combined - total) / LOG2E
    for copy in sent:
        copy.wait_send()


def rows_other(which, links, half, way):
    back = 1 - way
    if which == 0:
        return pl.ds(half + back * (1 - half), half)
    return pl.ds(links - back * links, 1)


def local_fast(points, potentials):
    times, pcs, cell_dev = points.shape
    links = times - 1
    tiles = lax.axis_size("tile")
    cells = tiles * cell_dev
    vmem = pl.BlockSpec(memory_space=pltpu.VMEM)
    dma = pltpu.SemaphoreType.DMA
    phases = links // 2 + 2
    line = tiles // 2
    return pl.pallas_call(
        functools.partial(chain_kernel, links, tiles),
        out_shape=jax.ShapeDtypeStruct((links // 2, 128), jnp.float32),
        in_specs=[vmem] * 2,
        out_specs=vmem,
        scratch_shapes=[
            pltpu.VMEM((times, tiles, pcs, 128), jnp.float32),
            pltpu.VMEM((tiles, times, 128), jnp.float32),
            pltpu.VMEM((256, cells), jnp.bfloat16),
            pltpu.VMEM((256, cells), jnp.bfloat16),
            pltpu.VMEM((cells, 256), jnp.bfloat16),
            pltpu.VMEM((cells, 256), jnp.bfloat16),
            pltpu.VMEM((cells, cells), jnp.float32),
            pltpu.VMEM((cells, cells), jnp.float32),
            pltpu.VMEM((times, 1, cells), jnp.float32),
            pltpu.VMEM((times, 1, cells), jnp.float32),
            pltpu.VMEM((1, cells), jnp.float32),
            pltpu.VMEM((cells, 128), jnp.float32),
            pltpu.VMEM((times, 1, 128), jnp.float32),
            pltpu.VMEM((times, 1, 128), jnp.float32),
            dma((phases, line)),
            dma((phases, line)),
            dma((phases, line)),
            dma((phases, line)),
            dma((links // 2,)),
            dma((links // 2,)),
            dma((2,)),
            dma((2,)),
        ],
        compiler_params=pltpu.CompilerParams(
            vmem_limit_bytes=48 * 1024 * 1024, collective_id=0, has_side_effects=True
        ),
    )(points, potentials)


def passed_along(block, axis, distance):
    devices = range(lax.axis_size(axis))
    route = [(i - distance, i) for i in devices if i - distance in devices]
    return lax.ppermute(block, axis, route)


def joined(part, axis, combine):
    gathered = jax.tree.map(lambda a: lax.all_gather(a, axis), part)

    def take(source):
        return jax.tree.map(lambda a: lax.dynamic_index_in_dim(a, source, 0, False), gathered)

    return lax.fori_loop(
        1, lax.axis_size(axis), lambda source, state: combine(state, take(source)), take(0)
    )


def pair_scores(source_pts, target_pts, source_msg):
    source_sq = jnp.sum(source_pts * source_pts, axis=0)
    target_sq = jnp.sum(target_pts * target_pts, axis=0)
    inner_prod = lax.dot_general(
        source_pts,
        target_pts,
        (((0,), (0,)), ((), ())),
        precision=lax.Precision.HIGHEST,
        preferred_element_type=jnp.float32,
    )
    pair_cost = source_sq[:, None] + target_sq[None, :] - 2.0 * inner_prod
    return source_msg[:, None] - pair_cost / EPSILON


def combine_lse(left_pair, right_pair):
    peak = jnp.maximum(left_pair[0], right_pair[0])
    return (
        peak,
        left_pair[1] * jnp.exp(left_pair[0] - peak) + right_pair[1] * jnp.exp(right_pair[0] - peak),
    )


def local(points, potentials):
    link_index = lax.axis_index("link")
    link_count = lax.axis_size("link")
    tile_count = lax.axis_size("tile")
    per_link = (points.shape[0] - 1) // link_count
    cell_dev = points.shape[2]
    total_cells = tile_count * cell_dev
    offset_link = link_index * per_link
    local_pts = lax.dynamic_slice_in_dim(points, offset_link, per_link + 1, 0)
    local_pot = lax.dynamic_slice_in_dim(potentials, offset_link, per_link + 1, 0)
    every_pts = lax.all_gather(local_pts, "tile", axis=2, tiled=True)

    def message(source_idx, target_idx, source_msg):
        source_pts = local_pts[source_idx]
        target_pot = local_pot[target_idx]
        target_all = every_pts[target_idx]
        scores = pair_scores(source_pts, target_all, source_msg)
        peak = jnp.max(scores, axis=0)
        partial_lse = peak + jnp.log(jnp.sum(jnp.exp(scores - peak[None, :]), axis=0))
        lse_parts = lax.all_to_all(
            partial_lse.reshape(tile_count, cell_dev),
            "tile",
            split_axis=0,
            concat_axis=0,
            tiled=True,
        )
        peak = jnp.max(lse_parts, axis=0)
        summed = jnp.sum(jnp.exp(lse_parts - peak[None, :]), axis=0)
        return target_pot + peak + jnp.log(summed)

    def sweep(start_msg, forward):
        start_pos = jnp.where(forward, 0, per_link).astype(jnp.int32)
        stored = jnp.zeros((per_link + 1, cell_dev), jnp.float32)
        stored = lax.dynamic_update_slice_in_dim(stored, start_msg[None, :], start_pos, 0)
        current = start_msg
        for link_step in range(per_link):
            source_idx = jnp.where(forward, link_step, per_link - link_step).astype(jnp.int32)
            target_idx = jnp.where(forward, link_step + 1, per_link - 1 - link_step).astype(
                jnp.int32
            )
            current = message(source_idx, target_idx, current)
            stored = lax.dynamic_update_slice_in_dim(stored, current[None, :], target_idx, 0)
        return stored

    first_end = link_index == 0
    early_pass = sweep(local_pot[0], True)
    handed = passed_along(early_pass[per_link], "link", 1)
    forward_msgs = sweep(jnp.where(first_end, local_pot[0], handed), True)
    late_pass = sweep(local_pot[per_link], False)
    handed_back = passed_along(late_pass[0], "link", -1)
    backward_msgs = sweep(jnp.where(first_end, handed_back, local_pot[per_link]), False)
    combined = forward_msgs + backward_msgs - local_pot
    last_row = combined[per_link]
    peak = jnp.max(last_row)
    summed = jnp.sum(jnp.exp(last_row - peak))
    peak, summed = joined((peak, summed), "tile", combine_lse)
    log_total = peak + jnp.log(summed)
    return -math.log(total_cells) - (combined[1:] - log_total)


def fits(mesh, points):
    times, pcs, total = points.shape
    cell_dev = total // (mesh.shape["groups"] * mesh.shape["tile"])
    cells = cell_dev * mesh.shape["tile"]
    held = 2 * cells * cells * 4 + 2 * times * cells * 32 * 4
    return (
        cell_dev == 128
        and pcs < 32
        and times % 2 == 1
        and mesh.shape["tile"] % 2 == 0
        and cells % STRIP == 0
        and mesh.shape["link"] == 2
        and held < 32 * 1024 * 1024
    )


def solution(mesh):
    placed = (P(None, None, ("groups", "tile")), P(None, ("groups", "tile")))

    def whole(points, potentials):
        body = local_fast if fits(mesh, points) else local
        return jax.shard_map(
            body, mesh=mesh, in_specs=placed, out_specs=P("link", ("groups", "tile")), check_vma=False
        )(points, potentials)

    return whole
```

profile of v0, /device:TPU:0, one launch (start us, length us, event | category | flops | bytes accessed | tf_op | source)
XLA Modules:
  0.0 37.5 jit_solution(8496342066594138706)
XLA Ops:
  0.0 0.0 copy-start
  0.0 0.9 %copy-done = f32[9,30,128]{2,1,0:T(8,128)S(1)} copy-done((f32[9,30,128]{2,1,0:T(8,128)S(1)}, f32[9,30,128]{2,1,0:T(8,128)}, u32[]{:S(2)}) %copy-start) | copy-done | bytes 138264
  0.9 0.0 copy-start.1
  0.9 0.7 %copy-done.1 = f32[9,128]{1,0:T(8,128)S(1)} copy-done((f32[9,128]{1,0:T(8,128)S(1)}, f32[9,128]{1,0:T(8,128)}, u32[]{:S(2)}) %copy-start.1) | copy-done | bytes 4632
  1.6 35.3 %shard_map.28 = f32[4,128]{1,0:T(4,128)S(1)} custom-call(f32[9,30,128]{2,1,0:T(8,128)S(1)} %copy-done, f32[9,128]{1,0:T(8,128)S(1)} %copy-done.1), custom_call_target="tpu_custom_call" | custom-call | tf_op jit(solution)/shard_map/pallas_call | solution.py:353
  36.9 0.6 %copy.4 = f32[4,128]{1,0:T(4,128)} copy(f32[4,128]{1,0:T(4,128)S(1)} %shard_map.28) | data formatting | bytes 4096
Async XLA Ops:
  0.0 0.9 %copy-start = (f32[9,30,128]{2,1,0:T(8,128)S(1)}, f32[9,30,128]{2,1,0:T(8,128)}, u32[]{:S(2)}) copy-start(f32[9,30,128]{2,1,0:T(8,128)} %pts.1) | copy-start | bytes 414724
  0.9 0.7 %copy-start.1 = (f32[9,128]{1,0:T(8,128)S(1)}, f32[9,128]{1,0:T(8,128)}, u32[]{:S(2)}) copy-start(f32[9,128]{1,0:T(8,128)} %pot.1) | copy-start | bytes 13828
where the time goes:
time: 37.7 us; the launch traced here: 37.5 us
  Pallas kernels  35.3 us (94%)
  local copies, waits for them, and re-layouts  2.19 us (6%)
    pallas_call x1, Pallas kernels, local_fast(): pl.pallas_call(functools.partial(chain_kernel, links, tiles), out_shape=j...  35.3 us
    unnamed x5, local copies, waits for them, and re-layouts  2.19 us

commit v1 on v0

--- a/solution.py
+++ b/solution.py
@@ -11,9 +11,11 @@
 EPSILON = 0.5
 LOG2E = math.log2(math.e)
 SCALE = 2.0 / EPSILON * LOG2E
-STRIP = 256
+STRIP = 1024
 ROWS = 8
 BLOCK = 64
+WAYS = 2
+DIRECT = 0
 
 
 def pieces(value):
@@ -32,12 +34,12 @@
 
 
 class Chain:
-    def __init__(self, links, tiles, pts, pot, right, left, score, alpha, const, rest, col, own, me, time):
+    def __init__(self, links, tiles, pts, pot, right, left, score, alpha, const, rest, col, own, tops, me, time):
         self.links, self.tiles = links, tiles
         self.pts, self.pot = pts, pot
         self.right, self.left, self.score = right, left, score
         self.alpha, self.const, self.rest = alpha, const, rest
-        self.col, self.own = col, own
+        self.col, self.own, self.tops = col, own, tops
         self.me, self.time = me, time
 
     def constants(self, k, r):
@@ -91,30 +93,39 @@
             self.left[slot][...], self.right[link % 2][:, lanes], preferred_element_type=jnp.float32
         )
 
+    def reduce_lanes(self, i):
+        for j in range(STRIP // ROWS):
+            rows = pl.ds(pl.multiple_of(i * STRIP + j * ROWS, ROWS), ROWS)
+            top = self.tops[rows, :]
+            peak = jnp.max(top, axis=1, keepdims=True)
+            total = jnp.sum(self.col[rows, :] * jnp.exp2(top - peak), axis=1, keepdims=True)
+            out = peak + jnp.log(total) * LOG2E
+            self.col[rows, :] = jnp.broadcast_to(out, (ROWS, 128))
+
     def message(self, link, i):
         t = self.time(link)
         after = self.time(link + 1)
         if link % 2 == 0:
             source = self.alpha[t]
+            rows = pl.ds(pl.multiple_of(i * STRIP, STRIP), STRIP)
+            dots = jnp.dot(self.left[(link // 2) % 2][rows, :], self.right[0][...], preferred_element_type=jnp.float32)
             tiles = [slice(j * 128, (j + 1) * 128) for j in range(self.tiles)]
             for j in range(STRIP // ROWS):
                 rows = pl.ds(pl.multiple_of(i * STRIP + j * ROWS, ROWS), ROWS)
-                s = [self.score[0][rows, c] + source[:, c] for c in tiles]
+                s = [dots[j * ROWS:(j + 1) * ROWS, c] + source[:, c] for c in tiles]
                 top = functools.reduce(jnp.maximum, s)
-                total = functools.reduce(jnp.add, [jnp.exp2(a - top) for a in s])
-                peak = jnp.max(top, axis=1, keepdims=True)
-                total = jnp.sum(total * jnp.exp2(top - peak), axis=1, keepdims=True)
-                out = peak + jnp.log(total) * LOG2E
-                self.col[rows, :] = jnp.broadcast_to(out, (ROWS, 128))
+                self.tops[rows, :] = top
+                self.col[rows, :] = functools.reduce(jnp.add, [jnp.exp2(a - top) for a in s])
         else:
             lanes = pl.ds(pl.multiple_of(i * STRIP, STRIP), STRIP)
             cells = self.col.shape[0]
             step = BLOCK
             peak = total = None
+            dots = jnp.dot(self.left[(link // 2) % 2][...], self.right[1][:, lanes], preferred_element_type=jnp.float32)
             for j in range(cells // step):
                 rows = slice(j * step, (j + 1) * step)
                 source = self.col[rows, :]
-                s = self.score[1][rows, lanes] + jnp.concatenate([source] * (STRIP // 128), axis=1)
+                s = dots[rows, :] + jnp.concatenate([source] * (STRIP // 128), axis=1)
                 s = s.reshape(step // 8, 8, STRIP)
                 top = jnp.max(s, axis=0)
                 if peak is None:
@@ -157,7 +168,6 @@
         share = self.tiles // turns
         ready(1)
         self.loop(self.tiles, lambda r: self.prep(0, r))
-        self.loop(turns, lambda i: self.product(0, i))
         ready(2)
         self.loop(self.tiles, lambda r: self.prep(1, r))
         for link in range(self.links):
@@ -166,13 +176,13 @@
 
             def body(i, link=link):
                 self.message(link, i)
-                if link + 1 < self.links:
-                    self.product(link + 1, i)
                 if link + 2 < self.links:
                     for j in range(share):
                         self.prep(link + 2, i * share + j)
 
             self.loop(turns, body)
+            if link % 2 == 0:
+                self.loop(turns, self.reduce_lanes)
             self.keep(link + 1)
             done(link + 1)
 
@@ -181,7 +191,8 @@
     held, pots, *pairs = scratch[:8]
     right, left, score = pairs[0:2], pairs[2:4], pairs[4:6]
     alpha, const, rest, col, own, other = scratch[8:14]
-    line_send, line_recv, pair_send, pair_recv, core_send, core_recv, end_send, end_recv = scratch[14:]
+    line_send, line_recv, pair_send, pair_recv, core_send, core_recv, end_send, end_recv = scratch[14:22]
+    fill, tops = scratch[22:]
     me = lax.axis_index("tile")
     way = lax.axis_index("link")
     line = tiles // 2
@@ -194,15 +205,16 @@
     ahead = lambda d: slot(lax.rem(at + d, line), side)
     behind = lambda d: lax.rem(at + line - d, line)
     chain = Chain(
-        links, tiles, held, pots, right, left, score, alpha, const, rest, col, own, me, time
+        links, tiles, held, pots, right, left, score, alpha, const, rest, col, own, tops, me, time
     )
 
-    def fill(t, carry):
-        held[t, me] = pts[t]
-        return carry
-
-    lax.fori_loop(0, links + 1, fill, 0)
-    pots[me] = pot[...]
+    early = pl.ds(way * half, half + 1)
+    mine = [
+        pltpu.make_async_copy(pot, pots.at[me], fill.at[0]),
+        pltpu.make_async_copy(pts.at[early], held.at[early, me], fill.at[1]),
+    ]
+    for copy in mine:
+        copy.start()
 
     barrier = pltpu.get_barrier_semaphore()
     peers = [{"tile": ahead(d)} for d in range(1, line)]
@@ -236,6 +248,12 @@
         copy.start()
         sent.append(copy)
 
+    def to_cross(c, d):
+        device = {"tile": slot(lax.rem(at + d, line), 1 - side)}
+        copy = remote(c, me, True, pair_send, pair_recv, d, device)
+        copy.start()
+        sent.append(copy)
+
     def to_pair(c, d):
         origin = slot(behind(d), side)
         copy = remote(c, origin, d == 0, pair_send, pair_recv, d, partner)
@@ -246,7 +264,8 @@
         for d in range(1, line):
             origin = slot(behind(d), side)
             remote(c, origin, False, line_send, line_recv, d, partner).wait_recv()
-            to_pair(c, d)
+            if c >= DIRECT:
+                to_pair(c, d)
 
     def arrive(c):
         for d in range(line):
@@ -289,11 +308,15 @@
 
     for c in range(len(chunks) + 1):
         for d in range(line - 1, 0, -1):
+            if c < DIRECT:
+                to_cross(c, d)
             to_line(c, d)
         to_pair(c, 0)
 
     def ready(k):
         if k == 1:
+            for copy in mine:
+                copy.wait()
             for c in range(4):
                 forward(c)
             for c in range(3):
@@ -324,11 +347,11 @@
     total = chain.log_total()
     ends(0, rows_other(0, links, half, way)).wait_recv()
     ends(1, rows_other(1, links, half, way)).wait_recv()
-    mine = pl.ds(pl.multiple_of(me * 128, 128), 128)
+    lanes = pl.ds(pl.multiple_of(me * 128, 128), 128)
     keep = -math.log(tiles * 128)
     for j in range(half):
         t = 1 + way * half + j
-        combined = own[t] + other[t] - const[t, :, mine]
+        combined = own[t] + other[t] - const[t, :, lanes]
         out[pl.ds(j, 1), :] = keep - (combined - total) / LOG2E
     for copy in sent:
         copy.wait_send()
@@ -347,13 +370,14 @@
     tiles = lax.axis_size("tile")
     cells = tiles * cell_dev
     vmem = pl.BlockSpec(memory_space=pltpu.VMEM)
+    hbm = pl.BlockSpec(memory_space=pltpu.HBM)
     dma = pltpu.SemaphoreType.DMA
     phases = links // 2 + 2
     line = tiles // 2
     return pl.pallas_call(
         functools.partial(chain_kernel, links, tiles),
         out_shape=jax.ShapeDtypeStruct((links // 2, 128), jnp.float32),
-        in_specs=[vmem] * 2,
+        in_specs=[hbm] * 2,
         out_specs=vmem,
         scratch_shapes=[
             pltpu.VMEM((times, tiles, pcs, 128), jnp.float32),
@@ -378,9 +402,11 @@
             dma((links // 2,)),
             dma((2,)),
             dma((2,)),
+            dma((2,)),
+            pltpu.VMEM((cells, 128), jnp.float32),
         ],
         compiler_params=pltpu.CompilerParams(
-            vmem_limit_bytes=48 * 1024 * 1024, collective_id=0, has_side_effects=True
+            vmem_limit_bytes=66900000, collective_id=0, has_side_effects=True
         ),
     )(points, potentials)
 

time: 37.7 us -> 32.1 us (0.85)
  Pallas kernels: 35.3 us -> 30.7 us
  local copies, waits for them, and re-layouts: 2.19 us -> 1.26 us
    pallas_call x1, Pallas kernels: 35.3 us -> 30.7 us  [local_fast(): pl.pallas_call(functools.partial(chain_kernel, links, tiles), out_shape=j...]
    unnamed x5 -> x1, local copies, waits for them, and re-layouts: 2.19 us -> 1.26 us
where the time goes in v1:
time: 32.1 us; the launch traced here: 31.9 us
  Pallas kernels  30.7 us (96%)
  local copies, waits for them, and re-layouts  1.26 us (4%)
    pallas_call x1, Pallas kernels, local_fast(): pl.pallas_call(functools.partial(chain_kernel, links, tiles), out_shape=j...  30.7 us
    unnamed x1, local copies, waits for them, and re-layouts  1.26 us

profile of v1, /device:TPU:0, one launch (start us, length us, event | category | flops | bytes accessed | tf_op | source)
XLA Modules:
  0.0 31.9 jit_solution(13396373614351435071)
XLA Ops:
  0.0 30.7 %shard_map.28 = f32[4,128]{1,0:T(4,128)} custom-call(f32[9,30,128]{2,1,0:T(8,128)} %pts.1, f32[9,128]{1,0:T(8,128)} %pot.1), custom_call_target="tpu_custom_call" | custom-call | tf_op jit(solution)/shard_map/pallas_call | solution.py:377
  30.7 1.3 %copy.4 = f32[4,128]{1,0:T(4,128)} copy(f32[4,128]{1,0:T(4,128)} %shard_map.28) | data formatting | bytes 4096

commit v2 on v1

--- a/solution.py
+++ b/solution.py
@@ -163,28 +163,32 @@
 
         lax.fori_loop(0, count, turn, 0)
 
+    def whole(self, action):
+        for r in range(self.tiles):
+            action(r)
+
     def run(self, ready, done):
-        turns = self.tiles * 128 // STRIP
-        share = self.tiles // turns
+        half = self.links // 2
+        ready(0)
+        self.whole(lambda r: self.constants(0, r))
+        self.whole(lambda r: self.prep_even(0, 0, r))
         ready(1)
-        self.loop(self.tiles, lambda r: self.prep(0, r))
-        ready(2)
-        self.loop(self.tiles, lambda r: self.prep(1, r))
+        self.whole(lambda r: self.constants(1, r))
+        self.whole(lambda r: self.prep_odd(1, r))
         for link in range(self.links):
-            if link + 3 <= self.links:
-                ready(link + 3)
-
-            def body(i, link=link):
-                self.message(link, i)
-                if link + 2 < self.links:
-                    for j in range(share):
-                        self.prep(link + 2, i * share + j)
-
-            self.loop(turns, body)
+            early = link + 1 < self.links and link >= half - 1
+            if early:
+                ready(link + 2)
+            self.message(link, 0)
+            if early:
+                self.whole(lambda r: self.prep(link + 1, r))
             if link % 2 == 0:
-                self.loop(turns, self.reduce_lanes)
+                self.reduce_lanes(0)
             self.keep(link + 1)
             done(link + 1)
+            if link + 1 < self.links and not early:
+                ready(link + 2)
+                self.whole(lambda r: self.prep(link + 1, r))
 
 
 def chain_kernel(links, tiles, pts, pot, out, *scratch):
@@ -314,18 +318,17 @@
         to_pair(c, 0)
 
     def ready(k):
-        if k == 1:
+        if k == 0:
             for copy in mine:
                 copy.wait()
             for c in range(4):
                 forward(c)
-            for c in range(3):
+            for c in range(2):
                 arrive(c)
-            across(1)
             across(0)
         elif k <= half:
-            if k < half:
-                forward(k + 2)
+            if k + 3 <= half + 1:
+                forward(k + 3)
             arrive(k + 1)
             if k < half:
                 across(k)
@@ -345,6 +348,9 @@
     chain.run(ready, done)
     chain.keep(0)
     total = chain.log_total()
+    last = sent.pop()
+    for copy in sent:
+        copy.wait_send()
     ends(0, rows_other(0, links, half, way)).wait_recv()
     ends(1, rows_other(1, links, half, way)).wait_recv()
     lanes = pl.ds(pl.multiple_of(me * 128, 128), 128)
@@ -353,8 +359,7 @@
         t = 1 + way * half + j
         combined = own[t] + other[t] - const[t, :, lanes]
         out[pl.ds(j, 1), :] = keep - (combined - total) / LOG2E
-    for copy in sent:
-        copy.wait_send()
+    last.wait_send()
 
 
 def rows_other(which, links, half, way):

time: 32.1 us -> 29.5 us (0.919)
  Pallas kernels: 30.7 us -> 28 us
    pallas_call x1, Pallas kernels: 30.7 us -> 28 us  [local_fast(): pl.pallas_call(functools.partial(chain_kernel, links, tiles), out_shape=j...]
where the time goes in v2:
time: 29.5 us; the launch traced here: 29.3 us
  Pallas kernels  28 us (95%)
  local copies, waits for them, and re-layouts  1.26 us (4%)
    pallas_call x1, Pallas kernels, local_fast(): pl.pallas_call(functools.partial(chain_kernel, links, tiles), out_shape=j...  28 us
    unnamed x1, local copies, waits for them, and re-layouts  1.26 us

profile of v2, /device:TPU:0, one launch (start us, length us, event | category | flops | bytes accessed | tf_op | source)
XLA Modules:
  0.0 29.3 jit_solution(8083627045019030902)
XLA Ops:
  0.0 28.0 %shard_map.28 = f32[4,128]{1,0:T(4,128)} custom-call(f32[9,30,128]{2,1,0:T(8,128)} %pts.1, f32[9,128]{1,0:T(8,128)} %pot.1), custom_call_target="tpu_custom_call" | custom-call | tf_op jit(solution)/shard_map/pallas_call | solution.py:382
  28.0 1.3 %copy.4 = f32[4,128]{1,0:T(4,128)} copy(f32[4,128]{1,0:T(4,128)} %shard_map.28) | data formatting | bytes 4096

commit v3 on v2

--- a/solution.py
+++ b/solution.py
@@ -14,8 +14,7 @@
 STRIP = 1024
 ROWS = 8
 BLOCK = 64
-WAYS = 2
-DIRECT = 0
+BAND = 256
 
 
 def pieces(value):
@@ -34,20 +33,20 @@
 
 
 class Chain:
-    def __init__(self, links, tiles, pts, pot, right, left, score, alpha, const, rest, col, own, tops, me, time):
+    def __init__(self, links, tiles, pcs, pts, right, left, score, alpha, const, rest, col, own, tops, at, place, time):
         self.links, self.tiles = links, tiles
-        self.pts, self.pot = pts, pot
+        self.pts, self.pcs = pts, pcs
         self.right, self.left, self.score = right, left, score
         self.alpha, self.const, self.rest = alpha, const, rest
         self.col, self.own, self.tops = col, own, tops
-        self.me, self.time = me, time
+        self.at, self.place, self.time = at, place, time
 
     def constants(self, k, r):
         t = self.time(k)
-        x = self.pts[t, r]
+        x = self.pts[t, self.place(r), : self.pcs]
         lanes = pl.ds(pl.multiple_of(r * 128, 128), 128)
         square = jnp.sum(x * x, axis=0, keepdims=True)
-        pot = self.pot[r, pl.ds(t, 1), :]
+        pot = self.pts[t, self.place(r), self.pcs :]
         self.const[t, :, lanes] = (pot - (2.0 / EPSILON) * square) * LOG2E
         if k == 0:
             self.alpha[t, :, lanes] = (pot - square / EPSILON) * LOG2E
@@ -55,7 +54,7 @@
             self.rest[:, lanes] = square * (LOG2E / EPSILON)
 
     def prep_even(self, k, link, r):
-        x = self.pts[self.time(k), r]
+        x = self.pts[self.time(k), self.place(r), : self.pcs]
         one = jnp.full((1, 128), 1.0 if link % 2 == 0 else 0.0, jnp.float32)
         h, m, l = pieces(padded(x, one))
         zero = jnp.zeros_like(h)
@@ -65,7 +64,7 @@
     def prep_odd(self, k, r):
         t = self.time(k)
         lanes = pl.ds(pl.multiple_of(r * 128, 128), 128)
-        x = padded(self.pts[t, r] * SCALE, self.const[t, :, lanes])
+        x = padded(self.pts[t, self.place(r), : self.pcs] * SCALE, self.const[t, :, lanes])
         h, m, l = pieces(x)
         block = jnp.concatenate([h, m, l, h], axis=0)
         block = block.T
@@ -102,20 +101,35 @@
             out = peak + jnp.log(total) * LOG2E
             self.col[rows, :] = jnp.broadcast_to(out, (ROWS, 128))
 
+    def partial(self, link, rows, tiles, first):
+        source = self.alpha[self.time(link)]
+        lanes = slice(tiles[0] * 128, tiles[-1] * 128 + 128)
+        for low in range(rows.start, rows.stop, BAND):
+            dots = jnp.dot(
+                self.left[(link // 2) % 2][low:low + BAND, :],
+                self.right[0][:, lanes],
+                preferred_element_type=jnp.float32,
+            )
+            for j in range(0, BAND, ROWS):
+                here = slice(low + j, low + j + ROWS)
+                s = [
+                    dots[j:j + ROWS, n * 128:n * 128 + 128] + source[:, c * 128:c * 128 + 128]
+                    for n, c in enumerate(tiles)
+                ]
+                top = functools.reduce(jnp.maximum, s)
+                if not first:
+                    old = self.tops[here, :]
+                    top = jnp.maximum(top, old)
+                total = functools.reduce(jnp.add, [jnp.exp2(a - top) for a in s])
+                if not first:
+                    total = total + self.col[here, :] * jnp.exp2(old - top)
+                self.tops[here, :] = top
+                self.col[here, :] = total
+
     def message(self, link, i):
-        t = self.time(link)
         after = self.time(link + 1)
         if link % 2 == 0:
-            source = self.alpha[t]
-            rows = pl.ds(pl.multiple_of(i * STRIP, STRIP), STRIP)
-            dots = jnp.dot(self.left[(link // 2) % 2][rows, :], self.right[0][...], preferred_element_type=jnp.float32)
-            tiles = [slice(j * 128, (j + 1) * 128) for j in range(self.tiles)]
-            for j in range(STRIP // ROWS):
-                rows = pl.ds(pl.multiple_of(i * STRIP + j * ROWS, ROWS), ROWS)
-                s = [dots[j * ROWS:(j + 1) * ROWS, c] + source[:, c] for c in tiles]
-                top = functools.reduce(jnp.maximum, s)
-                self.tops[rows, :] = top
-                self.col[rows, :] = functools.reduce(jnp.add, [jnp.exp2(a - top) for a in s])
+            self.partial(link, slice(0, self.tiles * 128), range(self.tiles), True)
         else:
             lanes = pl.ds(pl.multiple_of(i * STRIP, STRIP), STRIP)
             cells = self.col.shape[0]
@@ -141,7 +155,7 @@
 
     def keep(self, k):
         t = self.time(k)
-        mine = pl.ds(pl.multiple_of(self.me * 128, 128), 128)
+        mine = pl.ds(pl.multiple_of(self.at * 128, 128), 128)
         if k % 2 == 0:
             self.own[t] = self.alpha[t, :, mine]
         else:
@@ -163,23 +177,34 @@
 
         lax.fori_loop(0, count, turn, 0)
 
-    def whole(self, action):
-        for r in range(self.tiles):
+    def whole(self, action, low=0, high=None):
+        for r in range(low, self.tiles if high is None else high):
             action(r)
 
     def run(self, ready, done):
         half = self.links // 2
+        line = self.tiles // 2
+        near, far = slice(0, line * 128), slice(line * 128, self.tiles * 128)
         ready(0)
-        self.whole(lambda r: self.constants(0, r))
-        self.whole(lambda r: self.prep_even(0, 0, r))
+        self.whole(lambda r: self.constants(0, r), high=line)
+        self.whole(lambda r: self.prep_even(0, 0, r), high=line)
+        self.whole(lambda r: self.constants(1, r), high=line)
+        self.whole(lambda r: self.prep_odd(1, r), high=line)
+        self.partial(0, near, range(line), True)
+        ready("sources")
+        self.whole(lambda r: self.constants(0, r), low=line)
+        self.whole(lambda r: self.prep_even(0, 0, r), low=line)
+        self.partial(0, near, range(line, self.tiles), False)
         ready(1)
-        self.whole(lambda r: self.constants(1, r))
-        self.whole(lambda r: self.prep_odd(1, r))
+        self.whole(lambda r: self.constants(1, r), low=line)
+        self.whole(lambda r: self.prep_odd(1, r), low=line)
+        self.partial(0, far, range(self.tiles), True)
         for link in range(self.links):
             early = link + 1 < self.links and link >= half - 1
             if early:
                 ready(link + 2)
-            self.message(link, 0)
+            if link:
+                self.message(link, 0)
             if early:
                 self.whole(lambda r: self.prep(link + 1, r))
             if link % 2 == 0:
@@ -192,11 +217,11 @@
 
 
 def chain_kernel(links, tiles, pts, pot, out, *scratch):
-    held, pots, *pairs = scratch[:8]
+    held, *pairs = scratch[:7]
     right, left, score = pairs[0:2], pairs[2:4], pairs[4:6]
-    alpha, const, rest, col, own, other = scratch[8:14]
-    line_send, line_recv, pair_send, pair_recv, core_send, core_recv, end_send, end_recv = scratch[14:22]
-    fill, tops = scratch[22:]
+    alpha, const, rest, col, own, other = scratch[7:13]
+    line_send, line_recv, pair_send, pair_recv, core_send, core_recv, end_send, end_recv = scratch[13:21]
+    fill, tops, own_pts, own_pot, stage = scratch[21:]
     me = lax.axis_index("tile")
     way = lax.axis_index("link")
     line = tiles // 2
@@ -206,16 +231,17 @@
     time = lambda k: k + way * (links - 2 * k)
     first = lambda k, count: k + way * (links - 2 * k - count + 1)
     slot = lambda z, y: 2 * z + y
+    place = lambda r: slot(r % line, side if r < line else 1 - side)
     ahead = lambda d: slot(lax.rem(at + d, line), side)
     behind = lambda d: lax.rem(at + line - d, line)
     chain = Chain(
-        links, tiles, held, pots, right, left, score, alpha, const, rest, col, own, tops, me, time
+        links, tiles, pts.shape[1], held, right, left, score, alpha, const, rest, col, own, tops, at, place, time
     )
 
     early = pl.ds(way * half, half + 1)
     mine = [
-        pltpu.make_async_copy(pot, pots.at[me], fill.at[0]),
-        pltpu.make_async_copy(pts.at[early], held.at[early, me], fill.at[1]),
+        pltpu.make_async_copy(pot, own_pot, fill.at[0]),
+        pltpu.make_async_copy(pts.at[early], own_pts, fill.at[1]),
     ]
     for copy in mine:
         copy.start()
@@ -225,14 +251,20 @@
     peers += [{"tile": slot(at, 1 - side)}, {"link": 1 - way}]
     for peer in peers:
         pl.semaphore_signal(barrier, inc=1, device_id=peer)
+    for copy in mine:
+        copy.wait()
+    for j in range(half + 1):
+        t = way * half + j
+        block = jnp.concatenate([own_pts[j], own_pot[pl.ds(t, 1), :]], axis=0)
+        stage[j] = block
+        held[t, me] = block
     pl.semaphore_wait(barrier, len(peers))
 
     def views(c, origin, source_own):
-        if c == 0:
-            return (pot if source_own else pots.at[origin]), pots.at[origin]
-        k, count = chunks[c - 1]
+        k, count = chunks[c]
         span = pl.ds(first(k, count), count)
-        return (pts.at[span] if source_own else held.at[span, origin]), held.at[span, origin]
+        part = pl.ds(first(k, count) - way * half, count)
+        return (stage.at[part] if source_own else held.at[span, origin]), held.at[span, origin]
 
     def remote(c, origin, source_own, send, recv, d, device):
         src, dst = views(c, origin, source_own)
@@ -252,12 +284,6 @@
         copy.start()
         sent.append(copy)
 
-    def to_cross(c, d):
-        device = {"tile": slot(lax.rem(at + d, line), 1 - side)}
-        copy = remote(c, me, True, pair_send, pair_recv, d, device)
-        copy.start()
-        sent.append(copy)
-
     def to_pair(c, d):
         origin = slot(behind(d), side)
         copy = remote(c, origin, d == 0, pair_send, pair_recv, d, partner)
@@ -268,8 +294,7 @@
         for d in range(1, line):
             origin = slot(behind(d), side)
             remote(c, origin, False, line_send, line_recv, d, partner).wait_recv()
-            if c >= DIRECT:
-                to_pair(c, d)
+            to_pair(c, d)
 
     def arrive(c):
         for d in range(line):
@@ -310,56 +335,51 @@
             device_id={"link": 1 - way},
         )
 
-    for c in range(len(chunks) + 1):
+    for c in range(len(chunks)):
         for d in range(line - 1, 0, -1):
-            if c < DIRECT:
-                to_cross(c, d)
             to_line(c, d)
         to_pair(c, 0)
 
     def ready(k):
         if k == 0:
-            for copy in mine:
-                copy.wait()
-            for c in range(4):
+            for c in range(3):
                 forward(c)
-            for c in range(2):
-                arrive(c)
+        elif k == "sources":
+            arrive(0)
             across(0)
         elif k <= half:
-            if k + 3 <= half + 1:
-                forward(k + 3)
-            arrive(k + 1)
+            if k + 2 <= half:
+                forward(k + 2)
+            arrive(k)
             if k < half:
                 across(k)
-        else:
-            from_core(links - k)
+        elif k == half + 1:
+            for c in range(half - 1, -1, -1):
+                from_core(c)
 
     def done(k):
-        if k == links - 1:
-            copy = ends(0, rows(0))
-            copy.start()
-            sent.append(copy)
         if k == links:
-            copy = ends(1, rows(1))
-            copy.start()
-            sent.append(copy)
+            for which in range(2):
+                copy = ends(which, rows(which))
+                copy.start()
+                sent.append(copy)
 
     chain.run(ready, done)
     chain.keep(0)
     total = chain.log_total()
-    last = sent.pop()
+    last = [sent.pop(), sent.pop()]
     for copy in sent:
         copy.wait_send()
     ends(0, rows_other(0, links, half, way)).wait_recv()
     ends(1, rows_other(1, links, half, way)).wait_recv()
-    lanes = pl.ds(pl.multiple_of(me * 128, 128), 128)
+    lanes = pl.ds(pl.multiple_of(at * 128, 128), 128)
     keep = -math.log(tiles * 128)
     for j in range(half):
         t = 1 + way * half + j
         combined = own[t] + other[t] - const[t, :, lanes]
         out[pl.ds(j, 1), :] = keep - (combined - total) / LOG2E
-    last.wait_send()
+    for copy in last:
+        copy.wait_send()
 
 
 def rows_other(which, links, half, way):
@@ -377,7 +397,7 @@
     vmem = pl.BlockSpec(memory_space=pltpu.VMEM)
     hbm = pl.BlockSpec(memory_space=pltpu.HBM)
     dma = pltpu.SemaphoreType.DMA
-    phases = links // 2 + 2
+    phases = links // 2 + 1
     line = tiles // 2
     return pl.pallas_call(
         functools.partial(chain_kernel, links, tiles),
@@ -385,8 +405,7 @@
         in_specs=[hbm] * 2,
         out_specs=vmem,
         scratch_shapes=[
-            pltpu.VMEM((times, tiles, pcs, 128), jnp.float32),
-            pltpu.VMEM((tiles, times, 128), jnp.float32),
+            pltpu.VMEM((times, tiles, pcs + 1, 128), jnp.float32),
             pltpu.VMEM((256, cells), jnp.bfloat16),
             pltpu.VMEM((256, cells), jnp.bfloat16),
             pltpu.VMEM((cells, 256), jnp.bfloat16),
@@ -409,6 +428,9 @@
             dma((2,)),
             dma((2,)),
             pltpu.VMEM((cells, 128), jnp.float32),
+            pltpu.VMEM((links // 2 + 1, pcs, 128), jnp.float32),
+            pltpu.VMEM((times, 128), jnp.float32),
+            pltpu.VMEM((links // 2 + 1, pcs + 1, 128), jnp.float32),
         ],
         compiler_params=pltpu.CompilerParams(
             vmem_limit_bytes=66900000, collective_id=0, has_side_effects=True

time: 29.5 us -> 28.2 us (0.956)
  Pallas kernels: 28 us -> 26.7 us
    pallas_call x1, Pallas kernels: 28 us -> 26.7 us  [local_fast(): pl.pallas_call(functools.partial(chain_kernel, links, tiles), out_shape=j...]
where the time goes in v3:
time: 28.2 us; the launch traced here: 28 us
  Pallas kernels  26.7 us (95%)
  local copies, waits for them, and re-layouts  1.26 us (4%)
    pallas_call x1, Pallas kernels, local_fast(): pl.pallas_call(functools.partial(chain_kernel, links, tiles), out_shape=j...  26.7 us
    unnamed x1, local copies, waits for them, and re-layouts  1.26 us

profile of v3, /device:TPU:0, one launch (start us, length us, event | category | flops | bytes accessed | tf_op | source)
XLA Modules:
  0.0 28.0 jit_solution(4074280283769866726)
XLA Ops:
  0.0 26.7 %shard_map.28 = f32[4,128]{1,0:T(4,128)} custom-call(f32[9,30,128]{2,1,0:T(8,128)} %pts.1, f32[9,128]{1,0:T(8,128)} %pot.1), custom_call_target="tpu_custom_call" | custom-call | tf_op jit(solution)/shard_map/pallas_call | solution.py:402
  26.7 1.3 %copy.4 = f32[4,128]{1,0:T(4,128)} copy(f32[4,128]{1,0:T(4,128)} %shard_map.28) | data formatting | bytes 4096

commit v4 on v3

--- a/solution.py
+++ b/solution.py
@@ -25,18 +25,18 @@
     return high, middle, low
 
 
-def padded(points, extra):
+def padded(points, extra, slot):
     pad = 32 - points.shape[0]
     row = lax.broadcasted_iota(jnp.int32, (pad, points.shape[1]), 0)
-    tail = jnp.where(row == 0, 0.0 if extra is None else extra, 0.0)
+    tail = jnp.where(row == slot, extra, 0.0)
     return jnp.concatenate([points, tail], axis=0)
 
 
 class Chain:
-    def __init__(self, links, tiles, pcs, pts, right, left, score, alpha, const, rest, col, own, tops, at, place, time):
+    def __init__(self, links, tiles, pcs, pts, right, left, alpha, const, rest, col, own, tops, at, place, time):
         self.links, self.tiles = links, tiles
         self.pts, self.pcs = pts, pcs
-        self.right, self.left, self.score = right, left, score
+        self.right, self.left = right, left
         self.alpha, self.const, self.rest = alpha, const, rest
         self.col, self.own, self.tops = col, own, tops
         self.at, self.place, self.time = at, place, time
@@ -53,44 +53,30 @@
         if k == self.links:
             self.rest[:, lanes] = square * (LOG2E / EPSILON)
 
-    def prep_even(self, k, link, r):
+    def prep_even(self, k, r):
+        slot = (k // 2) % 2
         x = self.pts[self.time(k), self.place(r), : self.pcs]
-        one = jnp.full((1, 128), 1.0 if link % 2 == 0 else 0.0, jnp.float32)
-        h, m, l = pieces(padded(x, one))
-        zero = jnp.zeros_like(h)
+        h, m, l = pieces(padded(x, jnp.ones((1, 128), jnp.float32), slot))
         lanes = pl.ds(pl.multiple_of(r * 128, 128), 128)
-        self.right[link % 2][:, lanes] = jnp.concatenate([h, h, h, m, l, m, zero, zero], axis=0)
+        self.right[slot][0:192, lanes] = jnp.concatenate([h, h, h, m, l, m], axis=0)
 
     def prep_odd(self, k, r):
+        slot = (k // 2) % 2
         t = self.time(k)
         lanes = pl.ds(pl.multiple_of(r * 128, 128), 128)
-        x = padded(self.pts[t, self.place(r), : self.pcs] * SCALE, self.const[t, :, lanes])
-        h, m, l = pieces(x)
+        x = self.pts[t, self.place(r), : self.pcs] * SCALE
+        h, m, l = pieces(padded(x, self.const[t, :, lanes], slot))
         block = jnp.concatenate([h, m, l, h], axis=0)
         block = block.T
-        slot = (k // 2) % 2
         self.left[slot][lanes, 0:128] = block
         self.left[slot][lanes, 128:256] = block
 
     def prep(self, link, r):
+        self.constants(link + 1, r)
         if link % 2 == 0:
-            if link == 0:
-                self.constants(0, r)
-                self.prep_even(0, link, r)
-            else:
-                self.prep_even(link, link, r)
-            self.constants(link + 1, r)
             self.prep_odd(link + 1, r)
         else:
-            self.constants(link + 1, r)
-            self.prep_even(link + 1, link, r)
-
-    def product(self, link, i):
-        lanes = pl.ds(pl.multiple_of(i * STRIP, STRIP), STRIP)
-        slot = (link // 2) % 2
-        self.score[link % 2][:, lanes] = jnp.dot(
-            self.left[slot][...], self.right[link % 2][:, lanes], preferred_element_type=jnp.float32
-        )
+            self.prep_even(link + 1, r)
 
     def reduce_lanes(self, i):
         for j in range(STRIP // ROWS):
@@ -107,7 +93,7 @@
         for low in range(rows.start, rows.stop, BAND):
             dots = jnp.dot(
                 self.left[(link // 2) % 2][low:low + BAND, :],
-                self.right[0][:, lanes],
+                self.right[(link // 2) % 2][:, lanes],
                 preferred_element_type=jnp.float32,
             )
             for j in range(0, BAND, ROWS):
@@ -135,7 +121,7 @@
             cells = self.col.shape[0]
             step = BLOCK
             peak = total = None
-            dots = jnp.dot(self.left[(link // 2) % 2][...], self.right[1][:, lanes], preferred_element_type=jnp.float32)
+            dots = jnp.dot(self.left[(link // 2) % 2][...], self.right[((link + 1) // 2) % 2][:, lanes], preferred_element_type=jnp.float32)
             for j in range(cells // step):
                 rows = slice(j * step, (j + 1) * step)
                 source = self.col[rows, :]
@@ -187,13 +173,13 @@
         near, far = slice(0, line * 128), slice(line * 128, self.tiles * 128)
         ready(0)
         self.whole(lambda r: self.constants(0, r), high=line)
-        self.whole(lambda r: self.prep_even(0, 0, r), high=line)
+        self.whole(lambda r: self.prep_even(0, r), high=line)
         self.whole(lambda r: self.constants(1, r), high=line)
         self.whole(lambda r: self.prep_odd(1, r), high=line)
         self.partial(0, near, range(line), True)
         ready("sources")
         self.whole(lambda r: self.constants(0, r), low=line)
-        self.whole(lambda r: self.prep_even(0, 0, r), low=line)
+        self.whole(lambda r: self.prep_even(0, r), low=line)
         self.partial(0, near, range(line, self.tiles), False)
         ready(1)
         self.whole(lambda r: self.constants(1, r), low=line)
@@ -217,11 +203,11 @@
 
 
 def chain_kernel(links, tiles, pts, pot, out, *scratch):
-    held, *pairs = scratch[:7]
-    right, left, score = pairs[0:2], pairs[2:4], pairs[4:6]
-    alpha, const, rest, col, own, other = scratch[7:13]
-    line_send, line_recv, pair_send, pair_recv, core_send, core_recv, end_send, end_recv = scratch[13:21]
-    fill, tops, own_pts, own_pot, stage = scratch[21:]
+    held, *pairs = scratch[:5]
+    right, left = pairs[0:2], pairs[2:4]
+    alpha, const, rest, col, own, other = scratch[5:11]
+    line_send, line_recv, pair_send, pair_recv, core_send, core_recv, end_send, end_recv = scratch[11:19]
+    fill, tops, own_pts, own_pot, stage = scratch[19:]
     me = lax.axis_index("tile")
     way = lax.axis_index("link")
     line = tiles // 2
@@ -235,7 +221,7 @@
     ahead = lambda d: slot(lax.rem(at + d, line), side)
     behind = lambda d: lax.rem(at + line - d, line)
     chain = Chain(
-        links, tiles, pts.shape[1], held, right, left, score, alpha, const, rest, col, own, tops, at, place, time
+        links, tiles, pts.shape[1], held, right, left, alpha, const, rest, col, own, tops, at, place, time
     )
 
     early = pl.ds(way * half, half + 1)
@@ -258,6 +244,8 @@
         block = jnp.concatenate([own_pts[j], own_pot[pl.ds(t, 1), :]], axis=0)
         stage[j] = block
         held[t, me] = block
+    for buffer in right:
+        buffer[192:256, :] = jnp.zeros((64, tiles * 128), jnp.bfloat16)
     pl.semaphore_wait(barrier, len(peers))
 
     def views(c, origin, source_own):
@@ -410,8 +398,6 @@
             pltpu.VMEM((256, cells), jnp.bfloat16),
             pltpu.VMEM((cells, 256), jnp.bfloat16),
             pltpu.VMEM((cells, 256), jnp.bfloat16),
-            pltpu.VMEM((cells, cells), jnp.float32),
-            pltpu.VMEM((cells, cells), jnp.float32),
             pltpu.VMEM((times, 1, cells), jnp.float32),
             pltpu.VMEM((times, 1, cells), jnp.float32),
             pltpu.VMEM((1, cells), jnp.float32),
@@ -544,7 +530,7 @@
     held = 2 * cells * cells * 4 + 2 * times * cells * 32 * 4
     return (
         cell_dev == 128
-        and pcs < 32
+        and pcs < 31
         and times % 2 == 1
         and mesh.shape["tile"] % 2 == 0
         and cells % STRIP == 0

time: 28.2 us -> 27.9 us (0.989)
  no operation moved by 1% of the time
where the time goes in v4:
time: 27.9 us; the launch traced here: 27.7 us
  Pallas kernels  26.5 us (95%)
  local copies, waits for them, and re-layouts  1.26 us (5%)
    pallas_call x1, Pallas kernels, local_fast(): pl.pallas_call(functools.partial(chain_kernel, links, tiles), out_shape=j...  26.5 us
    unnamed x1, local copies, waits for them, and re-layouts  1.26 us

profile of v4, /device:TPU:0, one launch (start us, length us, event | category | flops | bytes accessed | tf_op | source)
XLA Modules:
  0.0 27.7 jit_solution(11722797029864825893)
XLA Ops:
  0.0 26.5 %shard_map.28 = f32[4,128]{1,0:T(4,128)} custom-call(f32[9,30,128]{2,1,0:T(8,128)} %pts.1, f32[9,128]{1,0:T(8,128)} %pot.1), custom_call_target="tpu_custom_call" | custom-call | tf_op jit(solution)/shard_map/pallas_call | solution.py:390
  26.5 1.3 %copy.4 = f32[4,128]{1,0:T(4,128)} copy(f32[4,128]{1,0:T(4,128)} %shard_map.28) | data formatting | bytes 4096
